TPU v7x, 32 devices: a whole 2x2x4 slice. The times are simulated.
32 devices in a mesh: row: 4 (over y, x), col: 8 (over z, core).
Axes of the slice: x: 2, y: 2, z: 4, core: 2. Of those that a mesh axis runs over, the one named last changes fastest.
Arguments:
- layer_input: bfloat16 [8192, 2048], P(('row', 'col')), may hold values from -6 to 6
- out_grad: bfloat16 [8192, 2048], P(('row', 'col')), may hold values from -6 to 6
- kv_grad: bfloat16 [8192, 256], P(('row', 'col')), may hold values from -6 to 6
- lengths: int32 [4, 4], P('row'), may hold values from 1 to 1024, 2048 in all within a row
- token_deal: int32 [4, 2048], P('row'), may hold values from 0 to 2047, each once within a row
- attn_gain: float32 [2048], P('row'), may hold values from 0.25 to 1.75
- query_weight: float32 [2048, 2048], P('row', 'col'), may hold values from -0.125 to 0.125
- key_weight: float32 [2048, 128], P('row'), may hold values from -0.125 to 0.125
- value_weight: float32 [2048, 128], P('row'), may hold values from -0.125 to 0.125
- out_weight: float32 [2048, 2048], P('col', 'row'), may hold values from -1 to 1
- mlp_gain: float32 [2048], P('row'), may hold values from 0.25 to 1.75
- gate_weight: float32 [2048, 5632], P('row', 'col'), may hold values from -0.125 to 0.125
- up_weight: float32 [2048, 5632], P('row', 'col'), may hold values from -0.125 to 0.125
- down_weight: float32 [5632, 2048], P('col', 'row'), may hold values from -0.3125 to 0.3125
Outputs:
- layer_output: bfloat16 [8192, 2048], P(('row', 'col'))
- input_grad: float32 [8192, 2048], P(('row', 'col'))
- shared_kv: bfloat16 [8192, 256], P(('row', 'col'))
- attn_gain_grad: float32 [2048], P('row')
- query_weight_grad: float32 [2048, 2048], P('row', 'col')
- key_weight_grad: float32 [2048, 128], P('row')
- value_weight_grad: float32 [2048, 128], P('row')
- out_weight_grad: float32 [2048, 2048], P('col', 'row')
- mlp_gain_grad: float32 [2048], P('row')
- gate_weight_grad: float32 [2048, 5632], P('row', 'col')
- up_weight_grad: float32 [2048, 5632], P('row', 'col')
- down_weight_grad: float32 [5632, 2048], P('col', 'row')
Inputs may be any that keep to these rules, and one draw needn't show every extreme that they name: Each row holds 4 lengths that sum to 2048; the longest of each row is exactly 1024. `token_deal`: each row is a permutation of 0 to 2047.
All inputs are finite; a program needn't handle non-finite values.
Results may differ from a plain program's by a relative error of at most 0.017.
The roundings to bfloat16 on the way count: a program that leaves them out, or rounds other values in their place, can miss the bound.
Values may be sent and summed in bfloat16 or wider, within the bound.
No kernel may reach another device: no remote copies, remote signals or barrier semaphores. Data moves between devices by JAX's collectives and lax.ppermute only.
A program may use at most 320 MiB of HBM per device.

v0:
```python
import jax
import jax.numpy as jnp
from jax import lax
from jax.sharding import PartitionSpec as P

norm_eps = 1e-05
rope_base = 10000.0
masked_score = -1e30


def rotate_pairs(values, positions, direction):
    half_dim = values.shape[-1] // 2
    frequency = rope_base ** (-jnp.arange(half_dim, dtype=jnp.float32) / half_dim)
    angles = positions.astype(jnp.float32)[:, None, None] * frequency
    cosine = jnp.cos(angles)
    sine_part = jnp.sin(angles) * direction
    first_half = values[..., :half_dim]
    second = values[..., half_dim:]
    return jnp.concatenate(
        [first_half * cosine - second * sine_part, second * cosine + first_half * sine_part],
        axis=-1,
    )


def norm_parts(values, gain):
    factor = lax.rsqrt(jnp.mean(values * values, axis=-1, keepdims=True) + norm_eps)
    return (factor, values * factor * gain)


def norm_backward(values, factor, gain, grad_rows):
    weighted = grad_rows * gain
    inner_mean = jnp.mean(weighted * values, axis=-1, keepdims=True)
    input_part = factor * weighted - values * factor * factor * factor * inner_mean
    gain_part = jnp.sum(grad_rows * values * factor, axis=0)
    return (input_part, gain_part)


def sequence_info(seq_lengths, group_rows):
    positions = jnp.arange(group_rows, dtype=jnp.int32)
    seq_ends = jnp.cumsum(seq_lengths)
    seq_ids = jnp.sum((positions[:, None] >= seq_ends[None, :]).astype(jnp.int32), axis=1)
    starts = jnp.sum(
        jnp.where(seq_ends[None, :] <= positions[:, None], seq_lengths[None, :], 0), axis=1
    )
    return (positions, seq_ids, positions - starts)


def block_scores(query_block, key_rows, seq_ids, first_row, block_rows, score_scale):
    key_index = jnp.arange(key_rows.shape[0], dtype=jnp.int32)
    row_index = first_row + jnp.arange(block_rows, dtype=jnp.int32)
    row_seq = lax.dynamic_slice_in_dim(seq_ids, first_row, block_rows, 0)
    scores = (
        jnp.einsum("qhd,kd->hqk", query_block, key_rows, preferred_element_type=jnp.float32)
        * score_scale
    )
    allowed = (row_seq[:, None] == seq_ids[None, :]) & (key_index[None, :] <= row_index[:, None])
    return jnp.where(allowed[None], scores, masked_score)


def attend_forward(queries, key_rows, value_rows, seq_ids):
    group_rows, head_count, head_dim = queries.shape
    block_rows = min(512, group_rows)
    score_scale = float(head_dim) ** (-0.5)
    count_blocks = group_rows // block_rows
    query_blocks = queries.reshape(count_blocks, block_rows, head_count, head_dim)
    first_rows = jnp.arange(count_blocks, dtype=jnp.int32) * block_rows

    def one_block(pieces):
        query_block, first_row = pieces
        scores = block_scores(query_block, key_rows, seq_ids, first_row, block_rows, score_scale)
        highest = jnp.max(scores, axis=-1, keepdims=True)
        exponent = jnp.exp(scores - highest)
        row_total = jnp.sum(exponent, axis=-1, keepdims=True)
        prob_low = (exponent / row_total).astype(jnp.bfloat16)
        mixed_rows = jnp.einsum(
            "hqk,kd->qhd", prob_low, value_rows, preferred_element_type=jnp.float32
        )
        return (mixed_rows.astype(jnp.bfloat16), (highest + jnp.log(row_total))[..., 0])

    mixed_rows, log_norm = lax.map(one_block, (query_blocks, first_rows))
    return (mixed_rows.reshape(group_rows, head_count, head_dim), log_norm)


def attend_backward(queries, key_rows, value_rows, seq_ids, mixed_grad, log_norm):
    group_rows, head_count, head_dim = queries.shape
    block_rows = min(512, group_rows)
    score_scale = float(head_dim) ** (-0.5)
    count_blocks = group_rows // block_rows
    query_blocks = queries.reshape(count_blocks, block_rows, head_count, head_dim)
    grad_blocks = mixed_grad.reshape(count_blocks, block_rows, head_count, head_dim)
    first_rows = jnp.arange(count_blocks, dtype=jnp.int32) * block_rows

    def one_block(carry, pieces):
        key_grad, value_grad = carry
        query_block, grad_block, norm_block, first_row = pieces
        scores = block_scores(query_block, key_rows, seq_ids, first_row, block_rows, score_scale)
        softmax_rows = jnp.exp(scores - norm_block[..., None])
        prob_low = softmax_rows.astype(jnp.bfloat16)
        prob_grad = jnp.einsum(
            "qhd,kd->hqk", grad_block, value_rows, preferred_element_type=jnp.float32
        )
        row_dot = jnp.sum(softmax_rows * prob_grad, axis=-1, keepdims=True)
        score_grad = (softmax_rows * (prob_grad - row_dot)).astype(jnp.bfloat16)
        query_grad = (
            jnp.einsum("hqk,kd->qhd", score_grad, key_rows, preferred_element_type=jnp.float32)
            * score_scale
        )
        key_grad = (
            key_grad
            + jnp.einsum("hqk,qhd->kd", score_grad, query_block, preferred_element_type=jnp.float32)
            * score_scale
        )
        value_grad = value_grad + jnp.einsum(
            "hqk,qhd->kd", prob_low, grad_block, preferred_element_type=jnp.float32
        )
        return ((key_grad, value_grad), query_grad)

    zero_rows = jnp.zeros((group_rows, head_dim), jnp.float32)
    (key_grad, value_grad), query_grad = lax.scan(
        one_block, (zero_rows, zero_rows), (query_blocks, grad_blocks, log_norm, first_rows)
    )
    return (query_grad.reshape(group_rows, head_count, head_dim), key_grad, value_grad)


def local(
    layer_input,
    out_grad,
    kv_grad,
    lengths,
    token_deal,
    attn_gain,
    query_weight,
    key_weight,
    value_weight,
    out_weight,
    mlp_gain,
    gate_weight,
    up_weight,
    down_weight,
):
    own_rows = layer_input.shape[0]
    col_index = lax.axis_index("col")
    group_rows = own_rows * lax.axis_size("col")
    head_dim = key_weight.shape[1]
    (
        gain_one,
        query_copy,
        key_copy,
        value_copy,
        out_copy,
        gain_two,
        gate_copy,
        up_copy,
        down_copy,
    ) = (
        lax.all_gather(attn_gain.astype(jnp.bfloat16), "row", axis=0, tiled=True),
        lax.all_gather(query_weight.astype(jnp.bfloat16), "row", axis=0, tiled=True),
        lax.all_gather(key_weight.astype(jnp.bfloat16), "row", axis=0, tiled=True),
        lax.all_gather(value_weight.astype(jnp.bfloat16), "row", axis=0, tiled=True),
        lax.all_gather(out_weight.astype(jnp.bfloat16), "row", axis=1, tiled=True),
        lax.all_gather(mlp_gain.astype(jnp.bfloat16), "row", axis=0, tiled=True),
        lax.all_gather(gate_weight.astype(jnp.bfloat16), "row", axis=0, tiled=True),
        lax.all_gather(up_weight.astype(jnp.bfloat16), "row", axis=0, tiled=True),
        lax.all_gather(down_weight.astype(jnp.bfloat16), "row", axis=1, tiled=True),
    )
    gain_one = gain_one.astype(jnp.float32)
    gain_two = gain_two.astype(jnp.float32)
    head_count = query_copy.shape[1] // head_dim
    positions, seq_ids, within = sequence_info(lengths[0], group_rows)
    slot_order = token_deal[0]
    inverse = jnp.zeros((group_rows,), jnp.int32).at[slot_order].set(positions)
    slot_pos = within[slot_order]
    own_pos = lax.dynamic_slice_in_dim(slot_pos, col_index * own_rows, own_rows, 0)
    input_rows = layer_input.astype(jnp.float32)
    factor_one, normed_one = norm_parts(input_rows, gain_one)
    normed_own = normed_one.astype(jnp.bfloat16)
    normed_rows, grad_rows = (
        lax.all_gather(normed_own, "col", axis=0, tiled=True),
        lax.all_gather(out_grad, "col", axis=0, tiled=True),
    )
    queries = jnp.dot(normed_rows, query_copy, preferred_element_type=jnp.float32).reshape(
        group_rows, head_count, head_dim
    )
    queries = rotate_pairs(queries, slot_pos, 1.0).astype(jnp.bfloat16)
    key_proj = jnp.dot(normed_rows, key_copy, preferred_element_type=jnp.float32)
    key_rows = rotate_pairs(key_proj[:, None, :], slot_pos, 1.0)[:, 0, :].astype(jnp.bfloat16)
    value_rows = jnp.dot(normed_rows, value_copy, preferred_element_type=jnp.float32).astype(
        jnp.bfloat16
    )
    shared_rows = jnp.concatenate([key_rows, value_rows], axis=1)
    shared_own = lax.dynamic_slice_in_dim(shared_rows, col_index * own_rows, own_rows, 0)
    query_orig = queries[inverse]
    key_orig = key_rows[inverse]
    value_orig = value_rows[inverse]
    mixed_orig, log_norm = attend_forward(query_orig, key_orig, value_orig, seq_ids)
    mixed_slot = mixed_orig[slot_order].reshape(group_rows, head_count * head_dim)
    out_full = lax.all_gather(out_copy, "col", axis=0, tiled=True)
    mixed_own = lax.all_to_all(mixed_slot, "col", split_axis=0, concat_axis=1, tiled=True)
    attended = jnp.dot(mixed_own, out_full, preferred_element_type=jnp.float32)
    middle = input_rows + attended
    factor_two, normed_two = norm_parts(middle, gain_two)
    mlp_rows = lax.all_gather(normed_two.astype(jnp.bfloat16), "col", axis=0, tiled=True)
    gate_act = jnp.dot(mlp_rows, gate_copy, preferred_element_type=jnp.float32)
    upward = jnp.dot(mlp_rows, up_copy, preferred_element_type=jnp.float32)
    sigmoid_gate = jax.nn.sigmoid(gate_act)
    silu_gate = gate_act * sigmoid_gate
    hidden = (silu_gate * upward).astype(jnp.bfloat16)
    output_rows = middle + lax.psum_scatter(
        jnp.dot(hidden, down_copy, preferred_element_type=jnp.float32),
        "col",
        scatter_dimension=0,
        tiled=True,
    )
    hidden_grad = jnp.dot(grad_rows, down_copy.T, preferred_element_type=jnp.float32)
    down_wgrad = jnp.dot(hidden.T, grad_rows, preferred_element_type=jnp.float32)
    gate_grad = (
        hidden_grad * upward * sigmoid_gate * (1.0 + gate_act * (1.0 - sigmoid_gate))
    ).astype(jnp.bfloat16)
    up_grad = (hidden_grad * silu_gate).astype(jnp.bfloat16)
    gate_wgrad = jnp.dot(mlp_rows.T, gate_grad, preferred_element_type=jnp.float32)
    up_wgrad = jnp.dot(mlp_rows.T, up_grad, preferred_element_type=jnp.float32)
    normed_two_grad = lax.psum_scatter(
        jnp.dot(gate_grad, gate_copy.T, preferred_element_type=jnp.float32)
        + jnp.dot(up_grad, up_copy.T, preferred_element_type=jnp.float32),
        "col",
        scatter_dimension=0,
        tiled=True,
    )
    middle_part, gain_two_grad = norm_backward(middle, factor_two, gain_two, normed_two_grad)
    middle_grad = out_grad.astype(jnp.float32) + middle_part
    middle_low = middle_grad.astype(jnp.bfloat16)
    middle_rows = lax.all_gather(middle_low, "col", axis=0, tiled=True)
    mixed_grad_slot = jnp.dot(middle_rows, out_copy.T, preferred_element_type=jnp.float32).astype(
        jnp.bfloat16
    )
    out_wgrad = jnp.dot(mixed_slot.T, middle_rows, preferred_element_type=jnp.float32)
    mixed_grad = mixed_grad_slot.reshape(group_rows, head_count, head_dim)[inverse]
    query_grad, key_grad, value_grad = attend_backward(
        query_orig, key_orig, value_orig, seq_ids, mixed_grad, log_norm
    )
    query_grad = (
        rotate_pairs(query_grad[slot_order], slot_pos, -1.0)
        .astype(jnp.bfloat16)
        .reshape(group_rows, head_count * head_dim)
    )
    query_wgrad = jnp.dot(normed_rows.T, query_grad, preferred_element_type=jnp.float32)
    shared_part = jnp.concatenate([key_grad, value_grad], axis=1)[slot_order]
    shared_cols = shared_part.shape[1]
    grad_parts = jnp.concatenate(
        [jnp.dot(query_grad, query_copy.T, preferred_element_type=jnp.float32), shared_part], axis=1
    )
    summed_parts = lax.psum_scatter(grad_parts, "col", scatter_dimension=0, tiled=True)
    width_cols = summed_parts.shape[1] - shared_cols
    normed_one_grad = summed_parts[:, :width_cols]
    shared_grad = summed_parts[:, width_cols:]
    shared_grad = shared_grad + kv_grad.astype(jnp.float32)
    key_own = rotate_pairs(shared_grad[:, None, :head_dim], own_pos, -1.0)[:, 0, :].astype(
        jnp.bfloat16
    )
    value_own = shared_grad[:, head_dim:].astype(jnp.bfloat16)
    key_wgrad = jnp.dot(normed_own.T, key_own, preferred_element_type=jnp.float32)
    value_wgrad = jnp.dot(normed_own.T, value_own, preferred_element_type=jnp.float32)
    normed_one_grad = (
        normed_one_grad
        + jnp.dot(key_own, key_copy.T, preferred_element_type=jnp.float32)
        + jnp.dot(value_own, value_copy.T, preferred_element_type=jnp.float32)
    )
    input_part, gain_one_grad = norm_backward(input_rows, factor_one, gain_one, normed_one_grad)
    input_grad = middle_grad + input_part
    summed = (
        lax.psum_scatter(gain_one_grad, "row", scatter_dimension=0, tiled=True),
        lax.psum_scatter(query_wgrad, "row", scatter_dimension=0, tiled=True),
        lax.psum_scatter(key_wgrad, "row", scatter_dimension=0, tiled=True),
        lax.psum_scatter(value_wgrad, "row", scatter_dimension=0, tiled=True),
        lax.psum_scatter(out_wgrad, "row", scatter_dimension=1, tiled=True),
        lax.psum_scatter(gain_two_grad, "row", scatter_dimension=0, tiled=True),
        lax.psum_scatter(gate_wgrad, "row", scatter_dimension=0, tiled=True),
        lax.psum_scatter(up_wgrad, "row", scatter_dimension=0, tiled=True),
        lax.psum_scatter(down_wgrad, "row", scatter_dimension=1, tiled=True),
    )
    gain_one_sum, key_sum, value_sum, gain_two_sum = lax.psum(
        (summed[0], summed[2], summed[3], summed[5]), "col"
    )
    return (
        output_rows.astype(jnp.bfloat16),
        input_grad,
        shared_own,
        gain_one_sum,
        summed[1],
        key_sum,
        value_sum,
        summed[4],
        gain_two_sum,
        summed[6],
        summed[7],
        summed[8],
    )


def solution(mesh):
    in_specs = (
        P(("row", "col"), None),
        P(("row", "col"), None),
        P(("row", "col"), None),
        P("row", None),
        P("row", None),
        P("row"),
        P("row", "col"),
        P("row", None),
        P("row", None),
        P("col", "row"),
        P("row"),
        P("row", "col"),
        P("row", "col"),
        P("col", "row"),
    )
    out_specs = (
        P(("row", "col"), None),
        P(("row", "col"), None),
        P(("row", "col"), None),
        P("row"),
        P("row", "col"),
        P("row", None),
        P("row", None),
        P("col", "row"),
        P("row"),
        P("row", "col"),
        P("row", "col"),
        P("col", "row"),
    )
    return jax.shard_map(local, mesh=mesh, in_specs=in_specs, out_specs=out_specs, check_vma=False)
```

profile of v0, /device:TPU:0, one launch (start us, length us, event | category | flops | bytes accessed | tf_op | source)
XLA Modules:
  0.0 1775.5 jit_solution(17734194517630113278)
XLA Ops:
  24.0 15.5 all-gather.17.cloned.1.call-done
  86.4 37.8 %all-gather.13.cloned.1.call-done = bf16[2048,2048]{0,1:T(8,128)(2,1)} async-done(((bf16[256,2048]{0,1:T(8,128)(2,1)}), bf16[2048,2048]{0,1:T(8,128)(2,1)}) %all-gather.13.cloned.1.call-update) | async-done | bytes 8388624 | tf_op jit(solution)/shard_map/all_gather | solution.py:178
  189.1 50.7 %while.27 = (s32[]{:T(128)}, bf16[4,512,2,128]{3,1,0,2:T(8,128)(2,1)}, f32[4,2,512]{2,1,0:T(2,128)S(1)}, s32[4]{0:T(128)S(1)}, s32[2048]{0:T(1024)S(1)}, /*index...) while((s32[]{:T(128)}, ...), condition=%wide.region_8.9_spmd, body=%wide.region_5.8_spmd.sunk | while | flops 1102183936 | bytes 30984376 | solution.py:80
  243.9 15.1 gather_fusion.4
  276.7 18.2 %all-to-all-done = bf16[8,256,256]{1,2,0:T(8,128)(2,1)S(1)} async-done(((bf16[8,256,256]{1,2,0:T(8,128)(2,1)}), bf16[8,256,256]{1,2,0:T(8,128)(2,1)S(1)}, u32[]{:S(2)}, u32[]{:S(2)}) %all-to-all-start) | async-done | bytes 1048608 | tf_op jit(solution)/shard_map/all_to_all | solution.py:198
  310.7 74.6 %all-gather.21.cloned.1.call-done = bf16[2048,2048]{0,1:T(8,128)(2,1)} async-done(((bf16[256,2048]{0,1:T(8,128)(2,1)}), bf16[2048,2048]{0,1:T(8,128)(2,1)}) %all-gather.21.cloned.1.call-update) | async-done | bytes 8388624 | tf_op jit(solution)/shard_map/all_gather | solution.py:202
  396.3 31.1 %all-gather.25.cloned.1.call-done = bf16[2048,704]{0,1:T(8,128)(2,1)} async-done(((bf16[512,704]{0,1:T(8,128)(2,1)}), bf16[2048,704]{0,1:T(8,128)(2,1)}) %all-gather.25.cloned.1.call-update) | async-done | bytes 2883600 | tf_op jit(solution)/shard_map/all_gather | solution.py:163
  438.5 32.4 %all-gather.27.cloned.1.call-done = bf16[704,2048]{1,0:T(8,128)(2,1)} async-done(((bf16[704,512]{1,0:T(8,128)(2,1)}), bf16[704,2048]{1,0:T(8,128)(2,1)}) %all-gather.27.cloned.1.call-update) | async-done | bytes 2883600 | tf_op jit(solution)/shard_map/all_gather | solution.py:164
  470.8 83.7 %all-gather.29.cloned.1.call-done = bf16[2048,2048]{1,0:T(8,128)(2,1)} async-done(((bf16[256,2048]{1,0:T(8,128)(2,1)}), bf16[2048,2048]{1,0:T(8,128)(2,1)}) %all-gather.29.cloned.1.call-update) | async-done | bytes 8388624 | tf_op jit(solution)/shard_map/all_gather | solution.py:179
  554.5 15.3 multiply_convert_fusion
  595.7 165.2 %reduce-scatter.13.cloned.1.call-done = f32[256,2048]{0,1:T(8,128)} async-done(((f32[2048,2048]{0,1:T(8,128)}), f32[256,2048]{0,1:T(8,128)}) %reduce-scatter.13.cloned.1.call-update) | async-done | bytes 2097168 | tf_op jit(solution)/shard_map/reduce_scatter | solution.py:222
  765.8 81.0 %all-gather.31.cloned.1.call-done = bf16[2048,2048]{0,1:T(8,128)(2,1)} async-done(((bf16[256,2048]{0,1:T(8,128)(2,1)}), bf16[2048,2048]{0,1:T(8,128)(2,1)}) %all-gather.31.cloned.1.call-update) | async-done | bytes 8388624 | tf_op jit(solution)/shard_map/all_gather | solution.py:232
  857.8 15.1 gather_fusion.5
  873.0 77.5 %while.28 = (s32[]{:T(128)}, f32[2048,128]{1,0:T(8,128)S(1)}, f32[2048,128]{1,0:T(8,128)}, f32[4,512,2,128]{3,1,0,2:T(8,128)}, s32[4]{0:T(128)S(1)}, /*index=5*/...) while((s32[]{:T(128)}, f32[2048,128]{1,0:T(8,128)S(1)}, ...), condition=%wide.region_15.16_spmd.clone, body=%wide.region_13.15_spmd.clone.sunk | while | flops 2720398848 | bytes 83409176 | solution.py:119
  955.3 14.5 gather_fusion.6
  1007.6 184.5 %reduce-scatter.15.cloned.1.call-done = f32[256,2304]{0,1:T(8,128)} async-done(((f32[2048,2304]{0,1:T(8,128)}), f32[256,2304]{0,1:T(8,128)}) %reduce-scatter.15.cloned.1.call-update) | async-done | bytes 2359312 | tf_op jit(solution)/shard_map/reduce_scatter | solution.py:252
  1267.7 154.9 %reduce-scatter.11.cloned.1.call-done = f32[256,2048]{0,1:T(8,128)} async-done(((f32[2048,2048]{0,1:T(8,128)}), f32[256,2048]{0,1:T(8,128)}) %reduce-scatter.11.cloned.1.call-update) | async-done | bytes 2097168 | tf_op jit(solution)/shard_map/reduce_scatter | solution.py:208
  1427.5 17.1 all-reduce.4
  1463.3 27.2 %reduce-scatter.29.cloned.1.call-done = f32[704,512]{1,0:T(8,128)} async-done(((f32[704,2048]{1,0:T(8,128)}), f32[704,512]{1,0:T(8,128)}) %reduce-scatter.29.cloned.1.call-update) | async-done | bytes 1441808 | tf_op jit(solution)/shard_map/reduce_scatter | solution.py:279
  1490.4 69.1 %reduce-scatter.25.cloned.1.call-done = f32[512,704]{0,1:T(8,128)} async-done(((f32[2048,704]{0,1:T(8,128)}), f32[512,704]{0,1:T(8,128)}) %reduce-scatter.25.cloned.1.call-update) | async-done | bytes 1441808 | tf_op jit(solution)/shard_map/reduce_scatter | solution.py:277
  1559.5 69.1 %reduce-scatter.27.cloned.1.call-done = f32[512,704]{0,1:T(8,128)} async-done(((f32[2048,704]{0,1:T(8,128)}), f32[512,704]{0,1:T(8,128)}) %reduce-scatter.27.cloned.1.call-update) | async-done | bytes 1441808 | tf_op jit(solution)/shard_map/reduce_scatter | solution.py:278
  1628.7 38.8 %reduce-scatter.17.cloned.1.call-done = f32[512,256]{1,0:T(8,128)} async-done(((f32[2048,256]{1,0:T(8,128)}), f32[512,256]{1,0:T(8,128)}) %reduce-scatter.17.cloned.1.call-update) | async-done | bytes 524304 | tf_op jit(solution)/shard_map/reduce_scatter | solution.py:272
  1667.4 38.6 %reduce-scatter.23.cloned.1.call-done = f32[256,512]{1,0:T(8,128)} async-done(((f32[256,2048]{1,0:T(8,128)}), f32[256,512]{1,0:T(8,128)}) %reduce-scatter.23.cloned.1.call-update) | async-done | bytes 524304 | tf_op jit(solution)/shard_map/reduce_scatter | solution.py:275
  1706.0 59.0 %all-reduce.7.cloned.1.call-done = (f32[512,128]{1,0:T(8,128)}, f32[512,128]{1,0:T(8,128)}) async-done(((f32[512,128]{1,0:T(8,128)}, f32[512,128]{1,0:T(8,128)}), (f32[512,128]{1,0:T(8,128)}, f32[512,128]{1,0:T(8,128)})) %all-reduce.7.cloned.1.call-update) | async-done | bytes 524304 | tf_op jit(solution)/shard_map/psum | solution.py:281
  (369 shorter events, 485.3 us)
Async XLA Ops:
  7.2 32.3 %all-gather.17.cloned.1.call-start = ((), (), s32[]{:S(2)}) async-start(), calls=%async_computation.13 | async-start | bytes 1310720 | tf_op jit(solution)/shard_map/all_gather | solution.py:160
  9.0 115.2 %all-gather.13.cloned.1.call-start = ((), (), s32[]{:S(2)}) async-start(), calls=%async_computation.11 | async-start | bytes 9437184 | tf_op jit(solution)/shard_map/all_gather | solution.py:178
  23.2 128.1 %all-gather.15.cloned.1.call-start = ((), (), s32[]{:S(2)}) async-start(), calls=%async_computation.12 | async-start | bytes 1310720 | tf_op jit(solution)/shard_map/all_gather | solution.py:157
  24.0 252.7 %all-gather.19.cloned.1.call-start = ((), (), s32[]{:S(2)}) async-start(), calls=%async_computation.14 | async-start | bytes 9437184 | tf_op jit(solution)/shard_map/all_gather | solution.py:197
  39.5 271.1 %all-gather.23.cloned.1.call-start = ((), (), s32[]{:S(2)}) async-start(), calls=%async_computation.16 | async-start | bytes 3604480 | tf_op jit(solution)/shard_map/all_gather | solution.py:162
  263.8 31.2 %all-to-all-start = ((bf16[8,256,256]{1,2,0:T(8,128)(2,1)}), bf16[8,256,256]{1,2,0:T(8,128)(2,1)S(1)}, u32[]{:S(2)}, u32[]{:S(2)}) async-start(bf16[8,256,256]{1,2,0:T(8,128)(2,1)} %copy.124), calls=%async_computation | async-start | bytes 2097152 | tf_op jit(solution)/shard_map/all_to_all | solution.py:198
  268.4 116.9 %all-gather.21.cloned.1.call-start = ((), (), s32[]{:S(2)}) async-start(), calls=%async_computation.15 | async-start | bytes 9437184 | tf_op jit(solution)/shard_map/all_gather | solution.py:202
  276.7 487.3 %copy-start.34 = (f32[4,1,512]{2,1,0:T(1,128)}, f32[4,1,512]{2,1,0:T(1,128)S(1)}, u32[]{:S(2)}) copy-start(f32[4,1,512]{2,1,0:T(1,128)S(1)} %convert_element_type.144) | copy-start | bytes 24580
  303.0 460.9 %copy-start = (f32[256,2048]{0,1:T(8,128)}, f32[256,2048]{0,1:T(8,128)S(1)}, u32[]{:S(2)}) copy-start(f32[256,2048]{0,1:T(8,128)S(1)} %get-tuple-element.395) | copy-start | bytes 6291460
  304.7 122.8 %all-gather.25.cloned.1.call-start = ((), (), s32[]{:S(2)}) async-start(), calls=%async_computation.17 | async-start | bytes 3604480 | tf_op jit(solution)/shard_map/all_gather | solution.py:163
  307.1 163.8 %all-gather.27.cloned.1.call-start = ((), (), s32[]{:S(2)}) async-start(), calls=%async_computation.18 | async-start | bytes 3604480 | tf_op jit(solution)/shard_map/all_gather | solution.py:164
  309.8 244.7 %all-gather.29.cloned.1.call-start = ((), (), s32[]{:S(2)}) async-start(), calls=%async_computation.20 | async-start | bytes 9437184 | tf_op jit(solution)/shard_map/all_gather | solution.py:179
  310.6 450.3 %reduce-scatter.13.cloned.1.call-start = ((), (), s32[]{:S(2)}) async-start(), calls=%async_computation.21 | async-start | bytes 18874368 | tf_op jit(solution)/shard_map/reduce_scatter | solution.py:222
  594.1 252.7 %all-gather.31.cloned.1.call-start = ((), (), s32[]{:S(2)}) async-start(), calls=%async_computation.22 | async-start | bytes 9437184 | tf_op jit(solution)/shard_map/all_gather | solution.py:232
  765.7 426.4 %reduce-scatter.15.cloned.1.call-start = ((), (), s32[]{:S(2)}) async-start(), calls=%async_computation.23 | async-start | bytes 21233664 | tf_op jit(solution)/shard_map/reduce_scatter | solution.py:252
  1005.9 261.8 %reduce-scatter.19.cloned.1.call-start = ((), (), s32[]{:S(2)}) async-start(), calls=%async_computation.25 | async-start | bytes 1310720 | tf_op jit(solution)/shard_map/reduce_scatter | solution.py:273
  1194.9 72.7 %reduce-scatter.21.cloned.1.call-start = ((), (), s32[]{:S(2)}) async-start(), calls=%async_computation.26 | async-start | bytes 1310720 | tf_op jit(solution)/shard_map/reduce_scatter | solution.py:274
  1196.4 226.1 %reduce-scatter.11.cloned.1.call-start = ((), (), s32[]{:S(2)}) async-start(), calls=%async_computation.19 | async-start | bytes 18874368 | tf_op jit(solution)/shard_map/reduce_scatter | solution.py:208
  1209.2 281.2 %reduce-scatter.29.cloned.1.call-start = ((), (), s32[]{:S(2)}) async-start(), calls=%async_computation.30 | async-start | bytes 7208960 | tf_op jit(solution)/shard_map/reduce_scatter | solution.py:279
  1220.4 339.1 %reduce-scatter.25.cloned.1.call-start = ((), (), s32[]{:S(2)}) async-start(), calls=%async_computation.28 | async-start | bytes 7208960 | tf_op jit(solution)/shard_map/reduce_scatter | solution.py:277
  1231.7 396.9 %reduce-scatter.27.cloned.1.call-start = ((), (), s32[]{:S(2)}) async-start(), calls=%async_computation.29 | async-start | bytes 7208960 | tf_op jit(solution)/shard_map/reduce_scatter | solution.py:278
  1243.0 424.5 %reduce-scatter.17.cloned.1.call-start = ((), (), s32[]{:S(2)}) async-start(), calls=%async_computation.24 | async-start | bytes 2621440 | tf_op jit(solution)/shard_map/reduce_scatter | solution.py:272
  1250.5 455.5 %reduce-scatter.23.cloned.1.call-start = ((), (), s32[]{:S(2)}) async-start(), calls=%async_computation.27 | async-start | bytes 2621440 | tf_op jit(solution)/shard_map/reduce_scatter | solution.py:275
  1260.1 505.0 %all-reduce.7.cloned.1.call-start = ((), (), s32[]{:S(2)}) async-start(), calls=%async_computation.31 | async-start | bytes 1048576 | tf_op jit(solution)/shard_map/psum | solution.py:281
  (65 other events, 2976.5 us)
Sparse Core Ops, SparseCore 0:
  10.4 29.0 all-gather.16
  41.7 82.4 all-gather.12
  126.6 24.6 all-gather.14
  152.8 82.0 all-gather.18
  236.5 40.0 all-gather.22
  304.8 80.4 all-gather.20
  387.7 39.7 all-gather.24
  429.3 41.5 all-gather.26
  472.4 82.0 all-gather.28
  594.2 166.6 reduce-scatter.12
  765.8 80.9 all-gather.30
  1006.0 186.0 reduce-scatter.14
  1195.0 26.3 reduce-scatter.18
  1224.2 27.9 reduce-scatter.20
  1254.4 168.1 reduce-scatter.10
  1426.0 64.4 reduce-scatter.28
  1493.8 65.6 reduce-scatter.24
  1563.0 65.6 reduce-scatter.26
  1632.2 35.1 reduce-scatter.16
  1670.8 35.1 reduce-scatter.22
  1708.4 56.5 all-reduce.6
where the time goes:
time: 1780 us
  waiting for transfers between devices  1180 us (66%)
  matrix products  230 us (13%)
  local copies, waits for them, and re-layouts  159 us (9%)
  other arithmetic  96.3 us (5%)
  blocking collectives  68.7 us (4%)
    reduce_scatter x1, waiting for transfers between devices, local(): lax.psum_scatter(grad_parts, 'col', scatter_dimension=0, tiled=True)  184 us
    reduce_scatter x1, waiting for transfers between devices, local(): lax.psum_scatter(jnp.dot(gate_grad, gate_copy.T, preferred_element_type=j...  165 us
    reduce_scatter x1, waiting for transfers between devices, local(): lax.psum_scatter(jnp.dot(hidden, down_copy, preferred_element_type=jnp.fl...  155 us
    all_gather x1, waiting for transfers between devices, local(): lax.all_gather(out_grad, 'col', axis=0, tiled=True)  83.7 us
    all_gather x1, waiting for transfers between devices, local(): middle_rows = lax.all_gather(middle_low, 'col', axis=0, tiled=True)  81 us
    all_gather x1, waiting for transfers between devices, local(): lax.all_gather(normed_two.astype(jnp.bfloat16), 'col', axis=0, tiled=True)  74.6 us
    reduce_scatter x1, waiting for transfers between devices, local(): lax.psum_scatter(up_wgrad, 'row', scatter_dimension=0, tiled=True)  69.1 us
    reduce_scatter x1, waiting for transfers between devices, local(): lax.psum_scatter(gate_wgrad, 'row', scatter_dimension=0, tiled=True)  69.1 us
  transfers between devices with their start and end apart: 22, of which 18 were waited for; matrix products, arithmetic and copies ran while one was open for 16% of the time, Pallas kernels for 0%

commit v1 on v0

--- a/solution.py
+++ b/solution.py
@@ -6,6 +6,12 @@
 norm_eps = 1e-05
 rope_base = 10000.0
 masked_score = -1e30
+
+
+def _shape_joints(array_here, in_dim):
+    odd = list(array_here.shape[1:])
+    odd[in_dim] *= array_here.shape[0]
+    return jnp.moveaxis(array_here, 0, in_dim).reshape(odd)
 
 
 def rotate_pairs(values, positions, direction):
@@ -229,7 +235,14 @@
     middle_part, gain_two_grad = norm_backward(middle, factor_two, gain_two, normed_two_grad)
     middle_grad = out_grad.astype(jnp.float32) + middle_part
     middle_low = middle_grad.astype(jnp.bfloat16)
-    middle_rows = lax.all_gather(middle_low, "col", axis=0, tiled=True)
+    n_shards = lax.axis_size("col")
+    table = [middle_low]
+    windows = [(rr, (rr + 1) % n_shards) for rr in range(n_shards)]
+    while len(table) < n_shards:
+        table.append(lax.ppermute(table[-1], "col", windows))
+    x_next = lax.axis_index("col")
+    table = jnp.stack(table)[(x_next - jnp.arange(n_shards)) % n_shards]
+    middle_rows = _shape_joints(table, 0)
     mixed_grad_slot = jnp.dot(middle_rows, out_copy.T, preferred_element_type=jnp.float32).astype(
         jnp.bfloat16
     )

time: 1780 us -> 1830 us (1.028)
  local copies, waits for them, and re-layouts: 159 us -> 189 us
  waiting for transfers between devices: 1180 us -> 1210 us
    ppermute x0 -> x7, waiting for transfers between devices: none -> 104 us  [local(): table.append(lax.ppermute(table[-1], 'col', windows))]
    all_gather x1 -> x0, waiting for transfers between devices: 81 us -> none  [local(): middle_rows = lax.all_gather(middle_low, 'col', axis=0, tiled=True)]
    gather x0 -> x2, local copies, waits for them, and re-layouts: none -> 19.7 us  [local(): table = jnp.stack(table)[(x_next - jnp.arange(n_shards)) % n_shards]]
  transfers between devices with their start and end apart: 22 -> 28, of which waited for: 18 -> 24; matrix products, arithmetic and copies ran while one was open for 16% -> 16% of each run, Pallas kernels for 0% -> 0%
where the time goes in v1:
time: 1830 us
  waiting for transfers between devices  1210 us (66%)
  matrix products  229 us (13%)
  local copies, waits for them, and re-layouts  189 us (10%)
  other arithmetic  96.4 us (5%)
  blocking collectives  68.6 us (4%)
    reduce_scatter x1, waiting for transfers between devices, local(): lax.psum_scatter(grad_parts, 'col', scatter_dimension=0, tiled=True)  184 us
    reduce_scatter x1, waiting for transfers between devices, local(): lax.psum_scatter(jnp.dot(gate_grad, gate_copy.T, preferred_element_type=j...  165 us
    reduce_scatter x1, waiting for transfers between devices, local(): lax.psum_scatter(jnp.dot(hidden, down_copy, preferred_element_type=jnp.fl...  155 us
    ppermute x7, waiting for transfers between devices, local(): table.append(lax.ppermute(table[-1], 'col', windows))  104 us
    all_gather x1, waiting for transfers between devices, local(): lax.all_gather(out_grad, 'col', axis=0, tiled=True)  83.7 us
    all_gather x1, waiting for transfers between devices, local(): lax.all_gather(normed_two.astype(jnp.bfloat16), 'col', axis=0, tiled=True)  74.6 us
    reduce_scatter x1, waiting for transfers between devices, local(): lax.psum_scatter(gate_wgrad, 'row', scatter_dimension=0, tiled=True)  69.1 us
    reduce_scatter x1, waiting for transfers between devices, local(): lax.psum_scatter(up_wgrad, 'row', scatter_dimension=0, tiled=True)  69.1 us
  transfers between devices with their start and end apart: 28, of which 24 were waited for; matrix products, arithmetic and copies ran while one was open for 16% of the time, Pallas kernels for 0%

profile of v1, /device:TPU:0, one launch (start us, length us, event | category | flops | bytes accessed | tf_op | source)
XLA Modules:
  0.0 1827.7 jit_solution(3670408259329383800)
XLA Ops:
  24.0 15.5 all-gather.16.cloned.1.call-done
  86.5 37.7 %all-gather.12.cloned.1.call-done = bf16[2048,2048]{0,1:T(8,128)(2,1)} async-done(((bf16[256,2048]{0,1:T(8,128)(2,1)}), bf16[2048,2048]{0,1:T(8,128)(2,1)}) %all-gather.12.cloned.1.call-update) | async-done | bytes 8388624 | tf_op jit(solution)/shard_map/all_gather | solution.py:184
  189.1 50.7 %while.27 = (s32[]{:T(128)}, bf16[4,512,2,128]{3,1,0,2:T(8,128)(2,1)}, f32[4,2,512]{2,1,0:T(2,128)S(1)}, s32[4]{0:T(128)S(1)}, s32[2048]{0:T(1024)S(1)}, /*index...) while((s32[]{:T(128)}, ...), condition=%wide.region_8.9_spmd, body=%wide.region_5.8_spmd.sunk | while | flops 1102183936 | bytes 30984376 | solution.py:86
  276.7 18.2 all-to-all-done
  310.7 74.6 %all-gather.20.cloned.1.call-done = bf16[2048,2048]{0,1:T(8,128)(2,1)} async-done(((bf16[256,2048]{0,1:T(8,128)(2,1)}), bf16[2048,2048]{0,1:T(8,128)(2,1)}) %all-gather.20.cloned.1.call-update) | async-done | bytes 8388624 | tf_op jit(solution)/shard_map/all_gather | solution.py:208
  396.3 31.1 %all-gather.24.cloned.1.call-done = bf16[2048,704]{0,1:T(8,128)(2,1)} async-done(((bf16[512,704]{0,1:T(8,128)(2,1)}), bf16[2048,704]{0,1:T(8,128)(2,1)}) %all-gather.24.cloned.1.call-update) | async-done | bytes 2883600 | tf_op jit(solution)/shard_map/all_gather | solution.py:169
  438.5 32.4 %all-gather.26.cloned.1.call-done = bf16[704,2048]{1,0:T(8,128)(2,1)} async-done(((bf16[704,512]{1,0:T(8,128)(2,1)}), bf16[704,2048]{1,0:T(8,128)(2,1)}) %all-gather.26.cloned.1.call-update) | async-done | bytes 2883600 | tf_op jit(solution)/shard_map/all_gather | solution.py:170
  470.8 83.7 %all-gather.28.cloned.1.call-done = bf16[2048,2048]{1,0:T(8,128)(2,1)} async-done(((bf16[256,2048]{1,0:T(8,128)(2,1)}), bf16[2048,2048]{1,0:T(8,128)(2,1)}) %all-gather.28.cloned.1.call-update) | async-done | bytes 8388624 | tf_op jit(solution)/shard_map/all_gather | solution.py:185
  595.6 165.3 %reduce-scatter.13.cloned.1.call-done = f32[256,2048]{0,1:T(8,128)} async-done(((f32[2048,2048]{0,1:T(8,128)}), f32[256,2048]{0,1:T(8,128)}) %reduce-scatter.13.cloned.1.call-update) | async-done | bytes 2097168 | tf_op jit(solution)/shard_map/reduce_scatter | solution.py:228
  765.6 16.0 collective-permute-done
  781.7 16.0 collective-permute-done.1
  797.7 16.0 collective-permute-done.2
  813.7 16.1 collective-permute-done.3
  829.9 16.3 collective-permute-done.4
  925.0 77.7 %while.28 = (s32[]{:T(128)}, f32[2048,128]{1,0:T(8,128)S(1)}, f32[2048,128]{1,0:T(8,128)}, f32[4,512,2,128]{3,1,0,2:T(8,128)}, s32[4]{0:T(128)S(1)}, /*index=5*/...) while((s32[]{:T(128)}, f32[2048,128]{1,0:T(8,128)S(1)}, ...), condition=%wide.region_15.16_spmd.clone, body=%wide.region_13.15_spmd.clone.sunk | while | flops 2720398848 | bytes 83409176 | solution.py:125
  1059.9 184.5 %reduce-scatter.15.cloned.1.call-done = f32[256,2304]{0,1:T(8,128)} async-done(((f32[2048,2304]{0,1:T(8,128)}), f32[256,2304]{0,1:T(8,128)}) %reduce-scatter.15.cloned.1.call-update) | async-done | bytes 2359312 | tf_op jit(solution)/shard_map/reduce_scatter | solution.py:265
  1319.7 155.3 %reduce-scatter.11.cloned.1.call-done = f32[256,2048]{0,1:T(8,128)} async-done(((f32[2048,2048]{0,1:T(8,128)}), f32[256,2048]{0,1:T(8,128)}) %reduce-scatter.11.cloned.1.call-update) | async-done | bytes 2097168 | tf_op jit(solution)/shard_map/reduce_scatter | solution.py:214
  1479.9 17.1 all-reduce.4
  1515.7 27.2 %reduce-scatter.29.cloned.1.call-done = f32[704,512]{1,0:T(8,128)} async-done(((f32[704,2048]{1,0:T(8,128)}), f32[704,512]{1,0:T(8,128)}) %reduce-scatter.29.cloned.1.call-update) | async-done | bytes 1441808 | tf_op jit(solution)/shard_map/reduce_scatter | solution.py:292
  1542.8 69.1 %reduce-scatter.25.cloned.1.call-done = f32[512,704]{0,1:T(8,128)} async-done(((f32[2048,704]{0,1:T(8,128)}), f32[512,704]{0,1:T(8,128)}) %reduce-scatter.25.cloned.1.call-update) | async-done | bytes 1441808 | tf_op jit(solution)/shard_map/reduce_scatter | solution.py:290
  1612.0 69.1 %reduce-scatter.27.cloned.1.call-done = f32[512,704]{0,1:T(8,128)} async-done(((f32[2048,704]{0,1:T(8,128)}), f32[512,704]{0,1:T(8,128)}) %reduce-scatter.27.cloned.1.call-update) | async-done | bytes 1441808 | tf_op jit(solution)/shard_map/reduce_scatter | solution.py:291
  1681.1 38.6 %reduce-scatter.17.cloned.1.call-done = f32[512,256]{1,0:T(8,128)} async-done(((f32[2048,256]{1,0:T(8,128)}), f32[512,256]{1,0:T(8,128)}) %reduce-scatter.17.cloned.1.call-update) | async-done | bytes 524304 | tf_op jit(solution)/shard_map/reduce_scatter | solution.py:285
  1719.7 38.7 %reduce-scatter.23.cloned.1.call-done = f32[256,512]{1,0:T(8,128)} async-done(((f32[256,2048]{1,0:T(8,128)}), f32[256,512]{1,0:T(8,128)}) %reduce-scatter.23.cloned.1.call-update) | async-done | bytes 524304 | tf_op jit(solution)/shard_map/reduce_scatter | solution.py:288
  1758.4 58.9 %all-reduce.7.cloned.1.call-done = (f32[512,128]{1,0:T(8,128)}, f32[512,128]{1,0:T(8,128)}) async-done(((f32[512,128]{1,0:T(8,128)}, f32[512,128]{1,0:T(8,128)}), (f32[512,128]{1,0:T(8,128)}, f32[512,128]{1,0:T(8,128)})) %all-reduce.7.cloned.1.call-update) | async-done | bytes 524304 | tf_op jit(solution)/shard_map/psum | solution.py:294
  (397 shorter events, 597.8 us)
Async XLA Ops:
  7.2 32.3 %all-gather.16.cloned.1.call-start = ((), (), s32[]{:S(2)}) async-start(), calls=%async_computation.13 | async-start | bytes 1310720 | tf_op jit(solution)/shard_map/all_gather | solution.py:166
  9.0 115.2 %all-gather.12.cloned.1.call-start = ((), (), s32[]{:S(2)}) async-start(), calls=%async_computation.11 | async-start | bytes 9437184 | tf_op jit(solution)/shard_map/all_gather | solution.py:184
  23.2 128.1 %all-gather.14.cloned.1.call-start = ((), (), s32[]{:S(2)}) async-start(), calls=%async_computation.12 | async-start | bytes 1310720 | tf_op jit(solution)/shard_map/all_gather | solution.py:163
  24.0 252.7 %all-gather.18.cloned.1.call-start = ((), (), s32[]{:S(2)}) async-start(), calls=%async_computation.14 | async-start | bytes 9437184 | tf_op jit(solution)/shard_map/all_gather | solution.py:203
  39.5 271.1 %all-gather.22.cloned.1.call-start = ((), (), s32[]{:S(2)}) async-start(), calls=%async_computation.16 | async-start | bytes 3604480 | tf_op jit(solution)/shard_map/all_gather | solution.py:168
  263.8 31.2 %all-to-all-start = ((bf16[8,256,256]{1,2,0:T(8,128)(2,1)}), bf16[8,256,256]{1,2,0:T(8,128)(2,1)S(1)}, u32[]{:S(2)}, u32[]{:S(2)}) async-start(bf16[8,256,256]{1,2,0:T(8,128)(2,1)} %copy.156), calls=%async_computation | async-start | bytes 2097152 | tf_op jit(solution)/shard_map/all_to_all | solution.py:204
  268.4 116.9 %all-gather.20.cloned.1.call-start = ((), (), s32[]{:S(2)}) async-start(), calls=%async_computation.15 | async-start | bytes 9437184 | tf_op jit(solution)/shard_map/all_gather | solution.py:208
  304.7 122.8 %all-gather.24.cloned.1.call-start = ((), (), s32[]{:S(2)}) async-start(), calls=%async_computation.17 | async-start | bytes 3604480 | tf_op jit(solution)/shard_map/all_gather | solution.py:169
  307.0 163.8 %all-gather.26.cloned.1.call-start = ((), (), s32[]{:S(2)}) async-start(), calls=%async_computation.18 | async-start | bytes 3604480 | tf_op jit(solution)/shard_map/all_gather | solution.py:170
  309.9 244.6 %all-gather.28.cloned.1.call-start = ((), (), s32[]{:S(2)}) async-start(), calls=%async_computation.20 | async-start | bytes 9437184 | tf_op jit(solution)/shard_map/all_gather | solution.py:185
  310.6 450.3 %reduce-scatter.13.cloned.1.call-start = ((), (), s32[]{:S(2)}) async-start(), calls=%async_computation.21 | async-start | bytes 18874368 | tf_op jit(solution)/shard_map/reduce_scatter | solution.py:228
  594.1 650.3 %reduce-scatter.15.cloned.1.call-start = ((), (), s32[]{:S(2)}) async-start(), calls=%async_computation.22 | async-start | bytes 21233664 | tf_op jit(solution)/shard_map/reduce_scatter | solution.py:265
  813.7 16.1 collective-permute-start.3
  829.8 16.3 collective-permute-start.4
  846.2 16.2 collective-permute-start.5
  1058.2 261.5 %reduce-scatter.19.cloned.1.call-start = ((), (), s32[]{:S(2)}) async-start(), calls=%async_computation.24 | async-start | bytes 1310720 | tf_op jit(solution)/shard_map/reduce_scatter | solution.py:286
  1247.1 72.5 %reduce-scatter.21.cloned.1.call-start = ((), (), s32[]{:S(2)}) async-start(), calls=%async_computation.25 | async-start | bytes 1310720 | tf_op jit(solution)/shard_map/reduce_scatter | solution.py:287
  1248.6 226.3 %reduce-scatter.11.cloned.1.call-start = ((), (), s32[]{:S(2)}) async-start(), calls=%async_computation.19 | async-start | bytes 18874368 | tf_op jit(solution)/shard_map/reduce_scatter | solution.py:214
  1261.4 281.4 %reduce-scatter.29.cloned.1.call-start = ((), (), s32[]{:S(2)}) async-start(), calls=%async_computation.29 | async-start | bytes 7208960 | tf_op jit(solution)/shard_map/reduce_scatter | solution.py:292
  1272.6 339.3 %reduce-scatter.25.cloned.1.call-start = ((), (), s32[]{:S(2)}) async-start(), calls=%async_computation.27 | async-start | bytes 7208960 | tf_op jit(solution)/shard_map/reduce_scatter | solution.py:290
  1283.9 397.1 %reduce-scatter.27.cloned.1.call-start = ((), (), s32[]{:S(2)}) async-start(), calls=%async_computation.28 | async-start | bytes 7208960 | tf_op jit(solution)/shard_map/reduce_scatter | solution.py:291
  1295.1 424.5 %reduce-scatter.17.cloned.1.call-start = ((), (), s32[]{:S(2)}) async-start(), calls=%async_computation.23 | async-start | bytes 2621440 | tf_op jit(solution)/shard_map/reduce_scatter | solution.py:285
  1302.6 455.8 %reduce-scatter.23.cloned.1.call-start = ((), (), s32[]{:S(2)}) async-start(), calls=%async_computation.26 | async-start | bytes 2621440 | tf_op jit(solution)/shard_map/reduce_scatter | solution.py:288
  1312.1 505.2 %all-reduce.7.cloned.1.call-start = ((), (), s32[]{:S(2)}) async-start(), calls=%async_computation.30 | async-start | bytes 1048576 | tf_op jit(solution)/shard_map/psum | solution.py:294
  (74 other events, 3953.5 us)
Sparse Core Ops, SparseCore 0:
  10.4 29.0 all-gather.15
  41.7 82.4 all-gather.11
  126.6 24.6 all-gather.13
  152.8 82.0 all-gather.17
  236.5 40.0 all-gather.21
  304.8 80.4 all-gather.19
  387.6 39.7 all-gather.23
  429.2 41.5 all-gather.25
  472.4 82.0 all-gather.27
  594.2 166.6 reduce-scatter.12
  1058.3 186.0 reduce-scatter.14
  1247.3 26.4 reduce-scatter.18
  1276.6 27.9 reduce-scatter.20
  1306.8 168.1 reduce-scatter.10
  1478.4 64.4 reduce-scatter.28
  1546.3 65.6 reduce-scatter.24
  1615.4 65.6 reduce-scatter.26
  1684.5 35.1 reduce-scatter.16
  1723.2 35.1 reduce-scatter.22
  1760.7 56.6 all-reduce.6
